TPU v7x, 32 devices: a whole 2x2x4 slice. The times are simulated.
32 devices in a mesh: prow: 4 (over y, x), pcol: 8 (over z, core).
Axes of the slice: x: 2, y: 2, z: 4, core: 2. Of those that a mesh axis runs over, the one named last changes fastest.
Arguments:
- covariance: float32 [16384, 16384], P(('prow', 'pcol')), may hold values from -600 to 600, as said below
- factor_left: float32 [64, 16384], P(None, ('prow', 'pcol')), may hold values from -6 to 6
- factor_right: float32 [64, 16384], P('prow', 'pcol'), may hold values from -3 to 3
Outputs:
- whitened: float32 [16384, 16384], P('prow', 'pcol')
Inputs may be any that keep to these rules, and one draw needn't show every extreme that they name: `covariance`: entries are real-valued and of full rank.
All inputs are finite; a program needn't handle non-finite values.
Results may differ from a plain program's by a relative error of at most 0.00007.
Values sent between devices are 32-bit elements; how exact they have to be, the bound alone decides.
A program may use at most 192 MiB of HBM per device.

v0:
```python
import jax
import jax.numpy as jnp
from jax import lax
from jax.sharding import PartitionSpec as P

ORDER = 16384
TILE = 64


epsilon = 1e-06


def deal_columns(source):
    height = source.shape[0]
    breadth = source.shape[1]
    grid_cols = lax.axis_size("pcol")
    arranged = (
        source.reshape(height, breadth // (TILE * grid_cols), grid_cols, TILE)
        .transpose(0, 2, 1, 3)
        .reshape(height, breadth)
    )
    return lax.all_to_all(arranged, "pcol", split_axis=1, concat_axis=0, tiled=True)


def order_rows(source):
    height = source.shape[0]
    breadth = source.shape[1]
    grid_rows = lax.axis_size("prow")
    grouped = source.reshape(height // (TILE * grid_rows), grid_rows, TILE, breadth)
    return grouped.transpose(1, 0, 2, 3).reshape(height, breadth)


def body(covariance, factor_left, factor_right):
    right_panel = lax.all_gather(factor_right, "prow", axis=0, tiled=True)
    dealt = deal_columns(covariance)
    left_block = lax.all_gather(factor_left, "pcol", axis=1, tiled=True).T
    tiles_moved, left_rows = (
        lax.all_to_all(order_rows(dealt), "prow", split_axis=0, concat_axis=0, tiled=True),
        lax.all_to_all(order_rows(left_block), "prow", split_axis=0, concat_axis=0, tiled=True),
    )
    corrected = tiles_moved + jnp.dot(
        left_rows, right_panel, precision=lax.Precision.HIGHEST, preferred_element_type=jnp.float32
    )
    squared = corrected * corrected
    row_total = lax.psum(jnp.sum(squared, axis=1), "pcol")
    col_total = lax.psum(jnp.sum(squared, axis=0), "prow")
    row_mean = row_total / ORDER + epsilon
    col_mean = col_total / ORDER + epsilon
    return corrected * lax.rsqrt(jnp.sqrt(row_mean[:, None] * col_mean[None, :]))


def solution(mesh):
    placed = (P(("prow", "pcol"), None), P(None, ("prow", "pcol")), P("prow", "pcol"))
    return jax.shard_map(
        body, mesh=mesh, in_specs=placed, out_specs=P("prow", "pcol"), check_vma=False
    )
```

profile of v0, /device:TPU:0, one launch (start us, length us, event | category | flops | bytes accessed | tf_op | source)
XLA Modules:
  0.0 1344.6 jit_solution(4344010486472771985)
XLA Ops:
  6.5 33.4 %copy.8 = f32[512,16384]{0,1:T(8,128)} copy(f32[512,16384]{1,0:T(8,128)} %param.3) | data formatting | bytes 67108864 | tf_op args[0]
  40.0 23.8 %copy.9 = f32[512,8,32,64]{0,3,2,1:T(8,128)} copy(f32[512,8,32,64]{0,3,1,2:T(8,128)} %bitcast.28) | data formatting | bytes 67108864 | tf_op jit(solution)/shard_map/transpose | solution.py:19
  63.7 7.1 all-to-all-start
  70.8 0.0 all-gather.2.cloned.1.call-start
  70.8 0.7 all-gather.2.cloned.1.call-update
  71.5 36.2 %all-gather.2.cloned.1.call-done = f32[64,4096]{1,0:T(8,128)} async-done(((f32[64,512]{1,0:T(8,128)}), f32[64,4096]{1,0:T(8,128)}) %all-gather.2.cloned.1.call-update) | async-done | bytes 1048592 | tf_op jit(solution)/shard_map/all_gather | solution.py:36
  107.8 2.6 reshape.27
  110.4 1.5 copy.16
  111.9 2.8 all_to_all.34
  114.6 688.7 %all-to-all-done = f32[512,8,2048]{0,2,1:T(8,128)} async-done(((f32[512,8,2048]{0,2,1:T(8,128)}), f32[512,8,2048]{0,2,1:T(8,128)}, u32[]{:S(2)}, u32[]{:S(2)}) %all-to-all-start) | async-done | bytes 33554464 | tf_op jit(solution)/shard_map/all_to_all | solution.py:22
  803.3 4.3 all-to-all-start.2
  807.6 31.7 %copy.10 = f32[8,512,2048]{2,1,0:T(8,128)} copy(f32[8,512,2048]{1,2,0:T(8,128)} %bitcast.3) | data formatting | bytes 67108864 | tf_op jit(solution)/shard_map/all_to_all | solution.py:22
  839.3 23.0 %copy.11 = f32[4,16,64,2048]{3,2,1,0:T(8,128)} copy(f32[4,16,64,2048]{3,2,0,1:T(8,128)} %bitcast.27) | data formatting | bytes 67108864 | tf_op jit(solution)/shard_map/transpose | solution.py:30
  862.3 0.0 all-to-all-done.2
  862.3 0.0 copy-start
  862.3 9.8 all-to-all-start.1
  872.1 0.0 copy-done
  872.2 367.5 %all_gather.7 = f32[64,2048]{1,0:T(8,128)S(1)} all-gather(f32[16,2048]{1,0:T(8,128)S(1)} %copy-done), channel_id=1, replica_groups=mesh['prow'=4,'pcol'=8] {'prow'}, dimensions={0}, use_global_device_ids=true | all-gather | bytes 655360 | tf_op jit(solution)/shard_map/all_gather | solution.py:34
  1239.6 0.1 copy.14
  1239.8 0.0 all-to-all-done.1
  1239.8 35.9 %multiply_reduce_fusion.1 = (f32[4096]{0:T(1024)S(1)}, f32[2048]{0:T(1024)S(1)}, f32[4096,2048]{1,0:T(8,128)}) fusion(f32[4096,64]{0,1:T(8,128)S(1)} %bitcast.30, f32[64,2048]{1,0:T(8,128)S(1)} %all_gather.7, f32[4,1024,2048]{2,1,0:T(8,128)} %all-to-all-done.1), kind=kOutput, calls=%fused_computation.3 | convolution fusion | flops 6475999232 | bytes 68706304 | tf_op jit(solution)/shard_map/dot_general | solution.py:41
  1275.6 25.9 %psum.14 = f32[4096]{0:T(1024)S(1)} all-reduce(f32[4096]{0:T(1024)S(1)} %get-tuple-element.5), channel_id=1, replica_groups=mesh['prow'=4,'pcol'=8] {'pcol'}, use_global_device_ids=true, to_apply=%region_1.0 | all-reduce | flops 4096 | bytes 32768 | tf_op jit(solution)/shard_map/psum | solution.py:45
  1301.5 9.1 psum.15
  1310.6 27.1 %rsqrt_multiply_fusion = f32[4096,2048]{1,0:T(8,128)} fusion(f32[4096,2048]{1,0:T(8,128)} %get-tuple-element.7, f32[2048]{0:T(1024)S(1)} %multiply_add_fusion.1, f32[4096]{0:T(1024)S(1)} %multiply_add_fusion), kind=kLoop, calls=%fused_computation.1 | loop fusion | flops 16777216 | bytes 67133440 | tf_op jit(solution)/shard_map/mul | solution.py:49
  (2 shorter events, 0.0 us)
Async XLA Ops:
  63.7 739.5 %all-to-all-start = ((f32[512,8,2048]{0,2,1:T(8,128)}), f32[512,8,2048]{0,2,1:T(8,128)}, u32[]{:S(2)}, u32[]{:S(2)}) async-start(f32[512,8,2048]{0,2,1:T(8,128)} %bitcast.25), calls=%async_computation | async-start | bytes 67108864 | tf_op jit(solution)/shard_map/all_to_all | solution.py:22
  70.8 36.9 %all-gather.2.cloned.1.call-start = ((), (), s32[]{:S(2)}) async-start(), calls=%async_computation.3 | async-start | bytes 1179648 | tf_op jit(solution)/shard_map/all_gather | solution.py:36
  803.3 59.0 %all-to-all-start.2 = ((f32[4,1024,64]{1,2,0:T(8,128)}), f32[4,1024,64]{1,2,0:T(8,128)S(1)}, u32[]{:S(2)}, u32[]{:S(2)}) async-start(f32[4,1024,64]{1,2,0:T(8,128)} %all_to_all.34), calls=%async_computation.2 | async-start | bytes 2097152 | tf_op jit(solution)/shard_map/all_to_all | solution.py:39
  862.3 9.8 copy-start
  862.3 377.4 %all-to-all-start.1 = ((f32[4,1024,2048]{2,1,0:T(8,128)}), f32[4,1024,2048]{2,1,0:T(8,128)}, u32[]{:S(2)}, u32[]{:S(2)}) async-start(f32[4,1024,2048]{2,1,0:T(8,128)} %bitcast.26), calls=%async_computation.1 | async-start | bytes 67108864 | tf_op jit(solution)/shard_map/all_to_all | solution.py:38
Sparse Core Ops, SparseCore 0:
  73.2 34.4 all-gather.1
where the time goes:
time: 1350 us; the launch traced here: 1340 us
  waiting for transfers between devices  726 us (54%)
  blocking collectives  402 us (30%)
  local copies, waits for them, and re-layouts  119 us (9%)
  matrix products  35.9 us (3%)
  other arithmetic  27.1 us (2%)
  starting transfers between devices  21.2 us (2%)
  between operations  13.5 us (1%)
    all_to_all x1, waiting for transfers between devices, deal_columns(): lax.all_to_all(arranged, 'pcol', split_axis=1, concat_axis=0, tiled=True)  689 us
    all_gather x1, blocking collectives, body(): right_panel = lax.all_gather(factor_right, 'prow', axis=0, tiled=True)  367 us
    all_gather x1, waiting for transfers between devices, body(): left_block = lax.all_gather(factor_left, 'pcol', axis=1, tiled=True).T  36.2 us
    dot_general x1, matrix products, body(): jnp.dot(left_rows, right_panel, precision=lax.Precision.HIGHEST, preferre...  35.9 us
    unnamed x3, local copies, waits for them, and re-layouts  33.4 us
    all_to_all x1, local copies, waits for them, and re-layouts, deal_columns(): lax.all_to_all(arranged, 'pcol', split_axis=1, concat_axis=0, tiled=True)  31.7 us
    mul x1, other arithmetic, body(): corrected * lax.rsqrt(jnp.sqrt(row_mean[:, None] * col_mean[None, :]))  27.1 us
  transfers between devices with their start and end apart: 4, of which 2 were waited for; matrix products, arithmetic and copies ran while one was open for 4% of the time, Pallas kernels for 0%

commit v1 on v0

--- a/solution.py
+++ b/solution.py
@@ -1,6 +1,10 @@
+import functools
+
 import jax
 import jax.numpy as jnp
 from jax import lax
+from jax.experimental import pallas as pl
+from jax.experimental.pallas import tpu as pltpu
 from jax.sharding import PartitionSpec as P
 
 ORDER = 16384
@@ -49,8 +53,209 @@
     return corrected * lax.rsqrt(jnp.sqrt(row_mean[:, None] * col_mean[None, :]))
 
 
+def flip(index, size, bits):
+    out, unit = 0, 1
+    while unit < size:
+        out = out + unit * ((index // unit + bits // unit) % 2)
+        unit *= 2
+    return out
+
+
+def deal_kernel(grid_cols, src, dst):
+    rows = src.shape[0]
+    low = lax.broadcasted_iota(jnp.int32, (rows, 2 * TILE), 1) < TILE
+    lanes = 2 * TILE
+    for pair in range(grid_cols // 2):
+        for m in range(src.shape[1] // (lanes * grid_cols)):
+            at = (pair + grid_cols * m) * lanes
+            first = src[:, at:at + lanes]
+            at += grid_cols // 2 * lanes
+            second = src[:, at:at + lanes]
+            dst[0, 2 * pair, :, m * lanes:(m + 1) * lanes] = jnp.where(low, first, pltpu.roll(second, TILE, 1))
+            dst[0, 2 * pair + 1, :, m * lanes:(m + 1) * lanes] = jnp.where(low, pltpu.roll(first, TILE, 1), second)
+
+
+def deal(covariance, grid_rows, grid_cols):
+    height, breadth = covariance.shape
+    tiles = height // TILE
+    step = TILE // 2
+    return pl.pallas_call(
+        functools.partial(deal_kernel, grid_cols),
+        grid=(tiles, TILE // step),
+        in_specs=[pl.BlockSpec((step, breadth), lambda j, h: (j * (TILE // step) + h, 0))],
+        out_specs=pl.BlockSpec(
+            (1, grid_cols, step, breadth // grid_cols),
+            lambda j, h: (j % grid_rows, 0, (j // grid_rows) * (TILE // step) + h, 0),
+        ),
+        out_shape=jax.ShapeDtypeStruct(
+            (grid_rows, grid_cols, height // grid_rows, breadth // grid_cols), jnp.float32
+        ),
+        compiler_params=pltpu.CompilerParams(vmem_limit_bytes=40 * 1024 * 1024),
+    )(covariance)
+
+
+def exchange_kernel(
+    grid_rows, grid_cols, tiles, left, right, got, got_left, got_right,
+    tile_send, tile_recv, left_send, left_recv, right_send, right_recv, swap_send, swap_recv, own,
+):
+    chips = grid_cols // 2
+    p = lax.axis_index("prow")
+    q = lax.axis_index("pcol")
+    z, core = q // 2, q % 2
+    height = tiles.shape[2]
+
+    def target(dp, dz, dc):
+        to_p = flip(p, grid_rows, dp)
+        to_q = 2 * flip(z, chips, dz) + (core + dc) % 2
+        return to_p, to_q
+
+    everyone = [
+        (dp, dz, dc)
+        for dz in [1] + list(range(chips - 1, 1, -1)) + [0]
+        for dp in range(grid_rows)
+        for dc in range(2)
+        if (dp, dz, dc) != (0, 0, 0)
+    ]
+    barrier = pltpu.get_barrier_semaphore()
+    for offset in everyone:
+        pl.semaphore_signal(barrier, inc=1, device_id=target(*offset), device_id_type=pl.DeviceIdType.MESH)
+    pl.semaphore_wait(barrier, len(everyone))
+
+    def copy(src, dst, send, recv, to):
+        return pltpu.make_async_remote_copy(
+            src_ref=src, dst_ref=dst, send_sem=send, recv_sem=recv,
+            device_id=to, device_id_type=pl.DeviceIdType.MESH,
+        )
+
+    my_slot = p * grid_cols + q
+    started = []
+    kept = [
+        pltpu.make_async_copy(left.at[p], got_left.at[core, p * chips + z], own.at[0]),
+        pltpu.make_async_copy(right, got_right.at[p], own.at[1]),
+    ]
+    for one in kept:
+        one.start()
+    lefts = []
+    for dz in range(chips):
+        for dp in range(grid_rows):
+            if (dp, dz) != (0, 0):
+                n = dz * grid_rows + dp
+                to = target(dp, dz, 0)
+                one = copy(left.at[to[0]], got_left.at[core, p * chips + z], left_send.at[n], left_recv.at[n], to)
+                one.start()
+                lefts.append(one)
+    for dp in range(1, grid_rows):
+        one = copy(right, got_right.at[p], right_send.at[dp], right_recv.at[dp], target(dp, 0, 0))
+        one.start()
+        started.append(one)
+    for n, offset in enumerate(everyone):
+        to = target(*offset)
+        one = copy(
+            tiles.at[to[0], to[1]], got.at[pl.ds(pl.multiple_of(my_slot * height, height), height)],
+            tile_send.at[n], tile_recv.at[n], to,
+        )
+        one.start()
+        started.append(one)
+    for one in kept:
+        one.wait()
+    for one in lefts:
+        one.wait()
+    swap = copy(got_left.at[core], got_left.at[core], swap_send, swap_recv, target(0, 0, 1))
+    swap.start()
+
+    piece = TILE // 2
+
+    def keep(scratch, sem_in, sem_out):
+        for n in range(height // piece):
+            one = pltpu.make_async_copy(tiles.at[p, q, pl.ds(n * piece, piece)], scratch.at[n], sem_in.at[n])
+            one.start()
+        for n in range(height // piece):
+            pltpu.make_async_copy(tiles.at[p, q, pl.ds(n * piece, piece)], scratch.at[n], sem_in.at[n]).wait()
+            pltpu.make_async_copy(
+                scratch.at[n], got.at[pl.ds(pl.multiple_of(my_slot * height + n * piece, piece), piece)], sem_out.at[n]
+            ).start()
+        for n in range(height // piece):
+            pltpu.make_async_copy(
+                scratch.at[n], got.at[pl.ds(pl.multiple_of(my_slot * height + n * piece, piece), piece)], sem_out.at[n]
+            ).wait()
+
+    pl.run_scoped(
+        keep,
+        pltpu.VMEM((height // piece, piece, tiles.shape[3]), jnp.float32),
+        pltpu.SemaphoreType.DMA((height // piece,)),
+        pltpu.SemaphoreType.DMA((height // piece,)),
+    )
+    swap.wait()
+    for one in started:
+        one.wait()
+
+
+def exchange(tiles, left, right):
+    grid_rows, grid_cols, height, breadth = tiles.shape
+    everyone = grid_rows * grid_cols
+    dma = pltpu.SemaphoreType.DMA
+    anywhere = pl.BlockSpec(memory_space=pl.ANY)
+    return pl.pallas_call(
+        functools.partial(exchange_kernel, grid_rows, grid_cols),
+        out_shape=(
+            jax.ShapeDtypeStruct((everyone * height, breadth), jnp.float32),
+            jax.ShapeDtypeStruct((2, everyone // 2) + left.shape[1:], jnp.float32),
+            jax.ShapeDtypeStruct((grid_rows,) + right.shape, jnp.float32),
+        ),
+        in_specs=[anywhere] * 3,
+        out_specs=(anywhere,) * 3,
+        scratch_shapes=[
+            dma((everyone,)), dma((everyone,)), dma((everyone // 2,)), dma((everyone // 2,)),
+            dma((grid_rows,)), dma((grid_rows,)), dma, dma, dma((2,)),
+        ],
+        compiler_params=pltpu.CompilerParams(collective_id=0, has_side_effects=True),
+    )(tiles, left, right)
+
+
+def direct_body(covariance, factor_left, factor_right):
+    grid_rows, grid_cols = lax.axis_size("prow"), lax.axis_size("pcol")
+    rank, height = factor_left.shape
+    each = height // grid_rows
+    tiles = deal(covariance, grid_rows, grid_cols)
+    left = (
+        factor_left.reshape(rank, each // TILE, grid_rows, TILE).transpose(2, 0, 1, 3).reshape(grid_rows, rank, each)
+    )
+    moved, lefts, rights = exchange(tiles, left, factor_right)
+    chips = grid_cols // 2
+    left_rows = (
+        lefts.reshape(2, grid_rows, chips, rank, each).transpose(1, 2, 0, 4, 3).reshape(-1, rank)
+    )
+    right_panel = rights.reshape(rank, -1)
+    corrected = moved + jnp.dot(
+        left_rows, right_panel, precision=lax.Precision.HIGHEST, preferred_element_type=jnp.float32
+    )
+    squared = corrected * corrected
+    row_total = lax.psum(jnp.sum(squared, axis=1), "pcol")
+    col_total = lax.psum(jnp.sum(squared, axis=0), "prow")
+    row_mean = row_total / ORDER + epsilon
+    col_mean = col_total / ORDER + epsilon
+    return corrected * lax.rsqrt(jnp.sqrt(row_mean[:, None] * col_mean[None, :]))
+
+
+def power_of_two(n):
+    return n & (n - 1) == 0
+
+
+def chosen(mesh, covariance):
+    grid_rows, grid_cols = mesh.shape["prow"], mesh.shape["pcol"]
+    tiles = covariance.shape[0] // (grid_rows * grid_cols * TILE)
+    fits = tiles > 0 and tiles % grid_rows == 0 and (tiles // grid_rows) % 2 == 0
+    across = covariance.shape[1] // (TILE * grid_cols)
+    fits = fits and power_of_two(grid_rows) and power_of_two(grid_cols) and grid_cols > 1 and across % 2 == 0
+    return direct_body if fits else body
+
+
 def solution(mesh):
     placed = (P(("prow", "pcol"), None), P(None, ("prow", "pcol")), P("prow", "pcol"))
-    return jax.shard_map(
-        body, mesh=mesh, in_specs=placed, out_specs=P("prow", "pcol"), check_vma=False
-    )
+
+    def run(covariance, factor_left, factor_right):
+        return jax.shard_map(
+            chosen(mesh, covariance), mesh=mesh, in_specs=placed, out_specs=P("prow", "pcol"), check_vma=False
+        )(covariance, factor_left, factor_right)
+
+    return run

time: 1350 us -> 1040 us (0.77)
  Pallas kernels: 0 us -> 935 us
  waiting for transfers between devices: 726 us -> 0 us
  blocking collectives: 402 us -> 36.9 us
  local copies, waits for them, and re-layouts: 119 us -> 4.9 us
  starting transfers between devices: 21.2 us -> 0 us
    pallas_call x0 -> x2, Pallas kernels: none -> 935 us  [the longest x1 904 us: exchange(): pl.pallas_call(functools.partial(exchange_kernel, grid_rows, grid_cols),...]
    all_to_all x3 -> x0, waiting for transfers between devices: 689 us -> none  [the longest x1 689 us: deal_columns(): lax.all_to_all(arranged, 'pcol', split_axis=1, concat_axis=0, tiled=True)]
    all_gather x1 -> x0, blocking collectives: 367 us -> none  [body(): right_panel = lax.all_gather(factor_right, 'prow', axis=0, tiled=True)]
    transpose x2 -> x0, local copies, waits for them, and re-layouts: 46.8 us -> none  [the longest x1 23.8 us: deal_columns(): arranged = source.reshape(height, breadth // (TILE * grid_cols), grid_col...]
    all_gather x1 -> x0, waiting for transfers between devices: 36.2 us -> none  [body(): left_block = lax.all_gather(factor_left, 'pcol', axis=1, tiled=True).T]
    all_to_all x3 -> x0, local copies, waits for them, and re-layouts: 34.5 us -> none  [the longest x1 31.7 us: deal_columns(): lax.all_to_all(arranged, 'pcol', split_axis=1, concat_axis=0, tiled=True)]
    unnamed x3 -> x0, local copies, waits for them, and re-layouts: 33.4 us -> none
    all_to_all x3 -> x0, starting transfers between devices: 21.2 us -> none  [the longest x1 9.82 us: body(): lax.all_to_all(order_rows(dealt), 'prow', split_axis=0, concat_axis=0, ti...]
  transfers between devices with their start and end apart: 4 -> 0, of which waited for: 2 -> 0; matrix products, arithmetic and copies ran while one was open for 4% -> 0% of each run, Pallas kernels for 0% -> 0%
where the time goes in v1:
time: 1040 us
  Pallas kernels  935 us (90%)
  matrix products  37.3 us (4%)
  blocking collectives  36.9 us (4%)
  other arithmetic  27.1 us (3%)
    pallas_call x1, Pallas kernels, exchange(): pl.pallas_call(functools.partial(exchange_kernel, grid_rows, grid_cols),...  904 us
    dot_general x1, matrix products, direct_body(): jnp.dot(left_rows, right_panel, precision=lax.Precision.HIGHEST, preferre...  37.3 us
    pallas_call x1, Pallas kernels, deal(): pl.pallas_call(functools.partial(deal_kernel, grid_cols), grid=(tiles, TI...  30.4 us
    psum x1, blocking collectives, direct_body(): row_total = lax.psum(jnp.sum(squared, axis=1), 'pcol')  27.5 us
    mul x1, other arithmetic, direct_body(): corrected * lax.rsqrt(jnp.sqrt(row_mean[:, None] * col_mean[None, :]))  27.1 us

profile of v1, /device:TPU:0, one launch (start us, length us, event | category | flops | bytes accessed | tf_op | source)
XLA Modules:
  0.0 1041.1 jit_solution(137068918945867578)
XLA Ops:
  0.0 1.1 reshape.17
  1.1 0.1 copy.10
  1.2 0.8 reshape.18.left
  2.0 30.4 %shard_map.37.tiles = f32[4,8,128,2048]{3,2,1,0:T(8,128)} custom-call(f32[512,16384]{1,0:T(8,128)} %src.1), custom_call_target="tpu_custom_call" | custom-call | tf_op jit(solution)/shard_map/pallas_call | solution.py:82
  32.4 904.5 %shard_map.38 = (f32[4096,2048]{1,0:T(8,128)}, f32[2,16,64,128]{3,2,1,0:T(8,128)}, f32[4,16,2048]{2,1,0:T(8,128)}) custom-call(f32[4,8,128,2048]{3,2,1,0:T(8,128)} %shard_map.37.tiles, f32[4,64,128]{2,1,0:T(8,128)} %reshape.18.left, f32[16,2048]{1,0:T(8,128)} %right.1), custom_call_target="tpu_custom_call" | custom-call | tf_op jit(solution)/shard_map/pallas_call | solution.py:198
  936.9 2.0 copy.9
  939.0 0.8 reshape.20
  939.8 37.3 %multiply_reduce_fusion.1 = (f32[4096]{0:T(1024)S(1)}, f32[2048]{0:T(1024)S(1)}, f32[4096,2048]{1,0:T(8,128)}) fusion(f32[4096,2048]{1,0:T(8,128)} %get-tuple-element.8, f32[4096,64]{0,1:T(8,128)S(1)} %reshape.20, f32[64,2048]{1,0:T(8,128)} %bitcast.15), kind=kOutput, calls=%fused_computation.2 | convolution fusion | flops 6475999232 | bytes 68706304 | tf_op jit(solution)/shard_map/dot_general | solution.py:229
  977.1 27.5 %psum.14 = f32[4096]{0:T(1024)S(1)} all-reduce(f32[4096]{0:T(1024)S(1)} %get-tuple-element.11), channel_id=1, replica_groups=mesh['prow'=4,'pcol'=8] {'pcol'}, use_global_device_ids=true, to_apply=%region_1.0 | all-reduce | flops 4096 | bytes 32768 | tf_op jit(solution)/shard_map/psum | solution.py:233
  1004.6 9.4 psum.15
  1014.0 27.1 %rsqrt_multiply_fusion = f32[4096,2048]{1,0:T(8,128)} fusion(f32[4096,2048]{1,0:T(8,128)} %get-tuple-element.13, f32[2048]{0:T(1024)S(1)} %multiply_add_fusion.1, f32[4096]{0:T(1024)S(1)} %multiply_add_fusion), kind=kLoop, calls=%fused_computation | loop fusion | flops 16777216 | bytes 67133440 | tf_op jit(solution)/shard_map/mul | solution.py:237
  (2 shorter events, 0.0 us)

commit v2 on v1

--- a/solution.py
+++ b/solution.py
@@ -109,12 +109,21 @@
         to_q = 2 * flip(z, chips, dz) + (core + dc) % 2
         return to_p, to_q
 
+    def offsets(distances):
+        return [
+            (dp, dz, dc)
+            for dp in range(grid_rows)
+            for dz in distances
+            for dc in range(2)
+            if (dp, dz, dc) != (0, 0, 0)
+        ]
+
+    across = offsets(range(chips - 1, chips // 2 - 1, -1))
+    within = offsets(range(chips // 2 - 1, -1, -1))
+    beside = (z + z // 2) % 2
     everyone = [
-        (dp, dz, dc)
-        for dz in [1] + list(range(chips - 1, 1, -1)) + [0]
-        for dp in range(grid_rows)
-        for dc in range(2)
-        if (dp, dz, dc) != (0, 0, 0)
+        tuple(beside * a + (1 - beside) * b for a, b in zip(first, second))
+        for first, second in zip(across + within, within + across)
     ]
     barrier = pltpu.get_barrier_semaphore()
     for offset in everyone:
@@ -150,9 +159,10 @@
         started.append(one)
     for n, offset in enumerate(everyone):
         to = target(*offset)
+        slot = (offset[0] * chips + offset[1]) * 2 + offset[2]
         one = copy(
             tiles.at[to[0], to[1]], got.at[pl.ds(pl.multiple_of(my_slot * height, height), height)],
-            tile_send.at[n], tile_recv.at[n], to,
+            tile_send.at[n], tile_recv.at[slot], to,
         )
         one.start()
         started.append(one)
@@ -227,7 +237,7 @@
     )
     right_panel = rights.reshape(rank, -1)
     corrected = moved + jnp.dot(
-        left_rows, right_panel, precision=lax.Precision.HIGHEST, preferred_element_type=jnp.float32
+        left_rows, right_panel, precision=lax.Precision.HIGH, preferred_element_type=jnp.float32
     )
     squared = corrected * corrected
     row_total = lax.psum(jnp.sum(squared, axis=1), "pcol")

time: 1040 us -> 871 us (0.84)
  Pallas kernels: 935 us -> 771 us
    pallas_call x1, Pallas kernels: 904 us -> 741 us  [exchange(): pl.pallas_call(functools.partial(exchange_kernel, grid_rows, grid_cols),...]
where the time goes in v2:
time: 871 us
  Pallas kernels  771 us (89%)
  blocking collectives  38.5 us (4%)
  matrix products  28.8 us (3%)
  other arithmetic  27.1 us (3%)
    pallas_call x1, Pallas kernels, exchange(): pl.pallas_call(functools.partial(exchange_kernel, grid_rows, grid_cols),...  741 us
    pallas_call x1, Pallas kernels, deal(): pl.pallas_call(functools.partial(deal_kernel, grid_cols), grid=(tiles, TI...  30.4 us
    dot_general x1, matrix products, direct_body(): jnp.dot(left_rows, right_panel, precision=lax.Precision.HIGH, preferred_e...  28.8 us
    psum x1, blocking collectives, direct_body(): row_total = lax.psum(jnp.sum(squared, axis=1), 'pcol')  28.4 us
    mul x1, other arithmetic, direct_body(): corrected * lax.rsqrt(jnp.sqrt(row_mean[:, None] * col_mean[None, :]))  27.1 us

profile of v2, /device:TPU:0, one launch (start us, length us, event | category | flops | bytes accessed | tf_op | source)
XLA Modules:
  0.0 870.7 jit_solution(7856806918280430099)
XLA Ops:
  0.0 1.1 reshape.17
  1.1 0.1 copy.10
  1.2 0.8 reshape.18.left
  2.0 30.4 %shard_map.37.tiles = f32[4,8,128,2048]{3,2,1,0:T(8,128)} custom-call(f32[512,16384]{1,0:T(8,128)} %src.1), custom_call_target="tpu_custom_call" | custom-call | tf_op jit(solution)/shard_map/pallas_call | solution.py:82
  32.4 741.0 %shard_map.38 = (f32[4096,2048]{1,0:T(8,128)}, f32[2,16,64,128]{3,2,1,0:T(8,128)}, f32[4,16,2048]{2,1,0:T(8,128)}) custom-call(f32[4,8,128,2048]{3,2,1,0:T(8,128)} %shard_map.37.tiles, f32[4,64,128]{2,1,0:T(8,128)} %reshape.18.left, f32[16,2048]{1,0:T(8,128)} %right.1), custom_call_target="tpu_custom_call" | custom-call | tf_op jit(solution)/shard_map/pallas_call | solution.py:208
  773.4 2.0 copy.9
  775.4 0.8 reshape.20
  776.3 28.8 %multiply_reduce_fusion.1 = (f32[4096]{0:T(1024)S(1)}, f32[2048]{0:T(1024)S(1)}, f32[4096,2048]{1,0:T(8,128)}) fusion(f32[4096,2048]{1,0:T(8,128)} %get-tuple-element.8, f32[4096,64]{0,1:T(8,128)S(1)} %reshape.20, f32[64,2048]{1,0:T(8,128)} %bitcast.15), kind=kOutput, calls=%fused_computation.2 | convolution fusion | flops 3254773760 | bytes 68706304 | tf_op jit(solution)/shard_map/dot_general | solution.py:239
  805.1 28.4 %psum.14 = f32[4096]{0:T(1024)S(1)} all-reduce(f32[4096]{0:T(1024)S(1)} %get-tuple-element.11), channel_id=1, replica_groups=mesh['prow'=4,'pcol'=8] {'pcol'}, use_global_device_ids=true, to_apply=%region_1.0 | all-reduce | flops 4096 | bytes 32768 | tf_op jit(solution)/shard_map/psum | solution.py:243
  833.4 10.1 %psum.15 = f32[2048]{0:T(1024)S(1)} all-reduce(f32[2048]{0:T(1024)S(1)} %get-tuple-element.12), channel_id=1, replica_groups=mesh['prow'=4,'pcol'=8] {'prow'}, use_global_device_ids=true, to_apply=%region_3.0 | all-reduce | flops 2048 | bytes 16384 | tf_op jit(solution)/shard_map/psum | solution.py:244
  843.6 27.1 %rsqrt_multiply_fusion = f32[4096,2048]{1,0:T(8,128)} fusion(f32[4096,2048]{1,0:T(8,128)} %get-tuple-element.13, f32[2048]{0:T(1024)S(1)} %multiply_add_fusion.1, f32[4096]{0:T(1024)S(1)} %multiply_add_fusion), kind=kLoop, calls=%fused_computation | loop fusion | flops 16777216 | bytes 67133440 | tf_op jit(solution)/shard_map/mul | solution.py:247
  (2 shorter events, 0.0 us)
